TPU v7x, 32 devices: a whole 2x2x4 slice. The times are simulated.
32 devices in a mesh: feat: 16 (over z, y, x), samp: 2 (over core).
Axes of the slice: x: 2, y: 2, z: 4, core: 2. Of those that a mesh axis runs over, the one named last changes fastest.
Arguments:
- features: bfloat16 [256, 131072], P('samp', 'feat'), may hold values from -14 to 14
- labels: int32 [256, 32], P('samp'), may hold values from -1 to 1, as said below
- alpha_start: float32 [256, 32], P('samp'), may hold values from 0 to 1
- order: int32 [2, 256], P(None, 'samp'), may hold values from 0 to 127, as said below
Outputs:
- alpha: float32 [256, 32], P('samp')
- scores: float32 [256, 32], P('samp')
Inputs may be any that keep to these rules, and one draw needn't show every extreme that they name: `labels`: every entry is -1 or +1. `order`: for each round, each aligned block of 128 entries (one partition) is a permutation of 0 to 127.
All inputs are finite; a program needn't handle non-finite values.
Results may differ from a plain program's by a relative error of at most 0.004.
Values may be sent and summed in bfloat16 or wider, within the bound.
A program may use at most 64 MiB of HBM per device.

v0:
```python
import jax
import jax.numpy as jnp
from jax import lax
from jax.sharding import PartitionSpec as P

BLOCK = 64
ROUNDS = 2


reg_scale = 0.9


def contract_rows(left_side, right_side):
    return lax.dot_general(
        left_side, right_side, (((0,), (0,)), ((), ())), preferred_element_type=jnp.float32
    )


def contract_cols(left_side, right_side):
    return lax.dot_general(
        left_side, right_side, (((1,), (1,)), ((), ())), preferred_element_type=jnp.float32
    )


def dual_update(before, margins, block_signs, block_norms, lam_total):
    return jnp.clip(
        before + lam_total * (1.0 - block_signs * margins) / block_norms[:, None], 0.0, 1.0
    )


def per_device(features, labels, alpha_start, order):
    row_count = features.shape[0]
    block_total = row_count // BLOCK
    part_count = lax.axis_size("samp")
    lam_total = reg_scale * features.shape[1] * lax.axis_size("feat")
    signs_all = labels.astype(jnp.float32)
    coeffs = (alpha_start * signs_all).astype(jnp.bfloat16)
    piece = (contract_rows(coeffs, features) / lam_total).astype(jnp.bfloat16)
    weights = lax.psum(piece, "samp").astype(jnp.float32)
    gram = lax.psum(contract_cols(features, features), "feat")
    norms_all = jnp.diagonal(gram) + 1.0
    alpha_now = alpha_start
    for round_num in range(ROUNDS):
        row_order = order[round_num]
        base = lax.psum(contract_cols(features, weights.astype(jnp.bfloat16)), "feat")

        def gram_block(block_num, carry, base=base, row_order=row_order):
            signed_total, local_alpha = carry
            chosen = lax.dynamic_slice_in_dim(row_order, block_num * BLOCK, BLOCK)
            coupling = jnp.dot(
                jnp.take(gram, chosen, axis=0), signed_total, precision=lax.Precision.HIGHEST
            )
            margins = jnp.take(base, chosen, axis=0) + coupling / lam_total
            before = jnp.take(local_alpha, chosen, axis=0)
            block_signs = jnp.take(signs_all, chosen, axis=0)
            updated = dual_update(
                before, margins, block_signs, jnp.take(norms_all, chosen, axis=0), lam_total
            )
            change = ((updated - before) * block_signs).astype(jnp.bfloat16)
            return (
                signed_total.at[chosen].add(change.astype(jnp.float32)),
                local_alpha.at[chosen].set(updated),
            )

        signed_total, local_alpha = lax.fori_loop(
            0, block_total, gram_block, (jnp.zeros_like(alpha_now), alpha_now)
        )
        delta_weights = (
            contract_rows(signed_total.astype(jnp.bfloat16), features) / lam_total
        ).astype(jnp.bfloat16)
        summed = lax.psum(delta_weights, "samp").astype(jnp.float32)
        weights = weights + summed / part_count
        alpha_now = alpha_now + (local_alpha - alpha_now) / part_count
    scores = lax.psum(contract_cols(features, weights.astype(jnp.bfloat16)), "feat")
    return (alpha_now, scores)


def solution(mesh):
    return jax.shard_map(
        per_device,
        mesh=mesh,
        in_specs=(P("samp", "feat"), P("samp", None), P("samp", None), P(None, "samp")),
        out_specs=(P("samp", None), P("samp", None)),
        check_vma=False,
    )
```

profile of v0, /device:TPU:0, one launch (start us, length us, event | category | flops | bytes accessed | tf_op | source)
XLA Modules:
  0.0 438.0 jit_solution(15617455799882391681)
XLA Ops:
  7.2 1.5 copy-done
  8.8 1.3 fusion.36
  10.4 1.3 fusion.24
  11.8 107.9 %all-reduce.7.cloned.1.call-done = f32[128,128]{1,0:T(8,128)} async-done(((f32[128,128]{1,0:T(8,128)}), f32[128,128]{1,0:T(8,128)}) %all-reduce.7.cloned.1.call-update) | async-done | bytes 65552 | tf_op jit(solution)/shard_map/psum | solution.py:40
  119.7 2.0 gather_fusion.10
  121.7 18.0 %all-reduce.5.cloned.1.call-done = bf16[32,8192]{1,0:T(8,128)(2,1)} async-done(((bf16[32,8192]{1,0:T(8,128)(2,1)}), bf16[32,8192]{1,0:T(8,128)(2,1)}) %all-reduce.5.cloned.1.call-update) | async-done | bytes 524304 | tf_op jit(solution)/shard_map/psum | solution.py:39
  139.7 1.8 convolution_bitcast_fusion.2
  141.6 77.1 %psum.50 = f32[128,32]{0,1:T(8,128)S(1)} all-reduce(f32[128,32]{0,1:T(8,128)S(1)} %convolution_bitcast_fusion.2), channel_id=1, replica_groups=mesh['feat'=16,'samp'=2] {'feat'}, use_global_device_ids=true, to_apply=%region_2.3 | all-reduce | flops 4096 | bytes 32768 | tf_op jit(solution)/shard_map/psum | solution.py:45
  218.7 11.5 %while.30 = (s32[]{:T(128)}, f32[128,32]{1,0:T(8,128)S(1)}, f32[128,32]{1,0:T(8,128)S(1)}, s32[128]{0:T(128)S(1)}, f32[128,32]{1,0:T(8,128)S(1)}, /*index=5*/f32...) while((s32[]{:T(128)}, f32[128,32]{1,0:T(8,128)S(1)}, ...), condition=%wide.region_6.0_spmd, body=%wide.region_3.9_spmd.sunk | while | flops 3188358 | bytes 344359 | solution.py:65
  222.6 1.0 scatter_fusion
  223.7 0.8 scatter_fusion.1
  228.4 1.0 scatter_fusion
  229.4 0.8 scatter_fusion.1
  230.2 1.3 fusion.25
  231.8 14.4 %all-reduce.9.cloned.1.call-done = bf16[32,8192]{1,0:T(8,128)(2,1)} async-done(((bf16[32,8192]{1,0:T(8,128)(2,1)}), bf16[32,8192]{1,0:T(8,128)(2,1)}) %all-reduce.9.cloned.1.call-update) | async-done | bytes 524304 | tf_op jit(solution)/shard_map/psum | solution.py:71
  246.2 1.9 convolution_bitcast_fusion.1
  248.0 77.0 %psum.53 = f32[128,32]{0,1:T(8,128)S(1)} all-reduce(f32[128,32]{0,1:T(8,128)S(1)} %convolution_bitcast_fusion.1), channel_id=1, replica_groups=mesh['feat'=16,'samp'=2] {'feat'}, use_global_device_ids=true, to_apply=%region_8.12 | all-reduce | flops 4096 | bytes 32768 | tf_op jit(solution)/shard_map/psum | solution.py:45
  325.2 11.5 %while.31 = (s32[]{:T(128)}, f32[128,32]{1,0:T(8,128)S(1)}, f32[128,32]{1,0:T(8,128)S(1)}, s32[128]{0:T(128)S(1)}, f32[128,32]{1,0:T(8,128)S(1)}, /*index=5*/f32...) while((s32[]{:T(128)}, f32[128,32]{1,0:T(8,128)S(1)}, ...), condition=%wide.region_12.16_spmd, body=%wide.region_9.15_spmd.sunk | while | flops 3188358 | bytes 344359 | solution.py:65
  329.1 1.0 scatter_fusion.2
  334.8 1.0 scatter_fusion.2
  336.7 1.3 fusion.26
  338.6 13.9 %all-reduce.11.cloned.1.call-done = bf16[32,8192]{1,0:T(8,128)(2,1)} async-done(((bf16[32,8192]{1,0:T(8,128)(2,1)}), bf16[32,8192]{1,0:T(8,128)(2,1)}) %all-reduce.11.cloned.1.call-update) | async-done | bytes 524304 | tf_op jit(solution)/shard_map/psum | solution.py:71
  352.6 1.9 convolution_bitcast_fusion
  354.5 77.0 %psum.55 = f32[128,32]{0,1:T(8,128)} all-reduce(f32[128,32]{0,1:T(8,128)S(1)} %convolution_bitcast_fusion), channel_id=1, replica_groups=mesh['feat'=16,'samp'=2] {'feat'}, use_global_device_ids=true, to_apply=%region_14.18 | all-reduce | flops 4096 | bytes 32768 | tf_op jit(solution)/shard_map/psum | solution.py:74
  (94 shorter events, 18.9 us)
Async XLA Ops:
  7.2 1.6 copy-start
  7.2 3.0 copy-start.5
  7.2 3.1 copy-start.4
  7.2 112.5 %all-reduce.7.cloned.1.call-start = ((), (), s32[]{:S(2)}) async-start(), calls=%async_computation.1 | async-start | bytes 131072 | tf_op jit(solution)/shard_map/psum | solution.py:40
  10.1 1.7 copy-start.6
  10.1 129.6 %all-reduce.5.cloned.1.call-start = ((), (), s32[]{:S(2)}) async-start(), calls=%async_computation | async-start | bytes 1048576 | tf_op jit(solution)/shard_map/psum | solution.py:39
  11.7 234.5 %all-reduce.9.cloned.1.call-start = ((), (), s32[]{:S(2)}) async-start(), calls=%async_computation.2 | async-start | bytes 1048576 | tf_op jit(solution)/shard_map/psum | solution.py:71
  119.7 99.0 %copy-start.1 = (f32[128,128]{1,0:T(8,128)S(1)}, f32[128,128]{1,0:T(8,128)}, u32[]{:S(2)}) copy-start(f32[128,128]{1,0:T(8,128)} %all-reduce.7.cloned.1.call-done) | copy-start | bytes 196612
  230.2 15.9 %copy-start.2 = (bf16[32,8192]{1,0:T(8,128)(2,1)S(1)}, bf16[32,8192]{1,0:T(8,128)(2,1)}, u32[]{:S(2)}) copy-start(bf16[32,8192]{1,0:T(8,128)(2,1)} %all-reduce.5.cloned.1.call-done) | copy-start | bytes 1572868
  231.5 121.1 %all-reduce.11.cloned.1.call-start = ((), (), s32[]{:S(2)}) async-start(), calls=%async_computation.3 | async-start | bytes 1048576 | tf_op jit(solution)/shard_map/psum | solution.py:71
  336.6 15.9 %copy-start.3 = (bf16[32,8192]{1,0:T(8,128)(2,1)S(1)}, bf16[32,8192]{1,0:T(8,128)(2,1)}, u32[]{:S(2)}) copy-start(bf16[32,8192]{1,0:T(8,128)(2,1)} %all-reduce.9.cloned.1.call-done) | copy-start | bytes 1572868
Sparse Core Ops, SparseCore 0:
  13.5 106.1 all-reduce.6
  122.0 17.6 all-reduce.4
  231.6 14.4 all-reduce.8
  338.1 14.4 all-reduce.10
where the time goes:
time: 438 us
  blocking collectives  231 us (53%)
  waiting for transfers between devices  154 us (35%)
  local copies, waits for them, and re-layouts  21.5 us (5%)
  between operations  13.9 us (3%)
  matrix products  11.9 us (3%)
  other arithmetic  4.86 us (1%)
    psum x3, blocking collectives, per_device(): lax.psum(contract_cols(features, weights.astype(jnp.bfloat16)), 'feat')  231 us
    psum x1, waiting for transfers between devices, per_device(): gram = lax.psum(contract_cols(features, features), 'feat')  108 us
    psum x2, waiting for transfers between devices, per_device(): summed = lax.psum(delta_weights, 'samp').astype(jnp.float32)  28.3 us
    psum x1, waiting for transfers between devices, per_device(): weights = lax.psum(piece, 'samp').astype(jnp.float32)  18 us
  transfers between devices with their start and end apart: 4, of which 4 were waited for; matrix products, arithmetic and copies ran while one was open for 1% of the time, Pallas kernels for 0%

commit v1 on v0

v1 whole, which is shorter than its diff:
```python
import functools

import jax
import jax.numpy as jnp
from jax import lax
from jax.experimental import pallas as pl
from jax.experimental.pallas import tpu as pltpu
from jax.sharding import PartitionSpec as P

BLOCK = 64
ROUNDS = 2
REG_SCALE = 0.9
PIECES = 2


def round_up(value, unit):
    return (value + unit - 1) // unit * unit


def gram_of(left, right):
    return lax.dot_general(
        left, right, (((1,), (1,)), ((), ())), preferred_element_type=jnp.float32
    )


def wrap(value, size):
    return lax.rem(value, size)


def kernel(
    feat_n, samp_n, lam_total,
    feats, labels, alphas, orders,
    alpha_out, score_out,
    own, shared, lab_all, alp_all, ord_all, part, inbox, full, ghl,
    load_sem, xs_sem, xr_sem, ms_sem, mr_sem, rs_send, rs_recv, ag_send, ag_recv, fw_send, fw_recv,
):
    rows, depth = feats.shape
    width = depth // samp_n
    piece = width // PIECES
    slab_a = part[0].shape[1]
    slab_b = part[1].shape[1] if len(part) > 1 else 0
    slabs = (slab_a, slab_b)
    starts = (0, slab_a)
    me_f, me_s = lax.axis_index("feat"), lax.axis_index("samp")

    barrier = pltpu.get_barrier_semaphore()
    for k in range(1, samp_n):
        pl.semaphore_signal(barrier, inc=1, device_id={"samp": wrap(me_s + k, samp_n)})
    for k in range(1, feat_n):
        pl.semaphore_signal(barrier, inc=1, device_id={"feat": wrap(me_f + k, feat_n)})

    def columns(owner, index):
        return pl.ds(pl.multiple_of(owner * width + index * piece, 128), piece)

    loads = []
    for k in range(samp_n):
        owner = wrap(me_s + k, samp_n)
        for i in range(PIECES):
            target = shared.at[me_s, i] if k == 0 else own.at[k - 1, i]
            loads.append(
                pltpu.make_async_copy(feats.at[:, columns(owner, i)], target, load_sem.at[k * PIECES + i])
            )
    for copy in loads:
        copy.start()
    smalls = ((labels, lab_all), (alphas, alp_all), (orders, ord_all))
    small_loads = [
        pltpu.make_async_copy(source, target.at[me_s], load_sem.at[samp_n * PIECES + n])
        for n, (source, target) in enumerate(smalls)
    ]
    for copy in small_loads:
        copy.start()

    pl.semaphore_wait(barrier, samp_n - 1 + feat_n - 1)

    exchange = []
    for k in range(1, samp_n):
        owner = wrap(me_s + k, samp_n)
        for i in range(PIECES):
            exchange.append(
                pltpu.make_async_remote_copy(
                    feats.at[:, columns(owner, i)], shared.at[me_s, i],
                    xs_sem.at[k - 1, i], xr_sem.at[me_s, i], device_id={"samp": owner},
                )
            )
    for k in range(1, samp_n):
        owner = wrap(me_s + k, samp_n)
        for n, (source, target) in enumerate(smalls):
            exchange.append(
                pltpu.make_async_remote_copy(
                    source, target.at[me_s], ms_sem.at[k - 1, n], mr_sem.at[me_s, n],
                    device_id={"samp": owner},
                )
            )
    for copy in exchange:
        copy.start()

    total = None
    for k in range(samp_n):
        for i in range(PIECES):
            loads[k * PIECES + i].wait()
            block = shared[me_s, i] if k == 0 else own[k - 1, i]
            term = gram_of(block, block)
            total = term if total is None else total + term

    scatter = []

    def scatter_out(group):
        size, start = slabs[group], starts[group]
        for k in range(1, feat_n):
            target = wrap(me_f + k, feat_n)
            copy = pltpu.make_async_remote_copy(
                part[group].at[target], inbox.at[me_f, pl.ds(start, size)],
                rs_send.at[group, k - 1], rs_recv.at[group, me_f], device_id={"feat": target},
            )
            copy.start()
            scatter.append(copy)

    def fill(group, value):
        size = slabs[group]
        count = feat_n * size
        if value.shape[0] < count:
            value = jnp.concatenate(
                [value, jnp.zeros((count - value.shape[0], rows), jnp.float32)], axis=0
            )
        part[group][...] = value.reshape(feat_n, size, rows)

    fill(0, total)
    scatter_out(0)

    pairs = [(p, q) for p in range(samp_n) for q in range(p + 1, samp_n)]
    if pairs:
        cross = [None] * len(pairs)
        for i in range(PIECES):
            for k in range(1, samp_n):
                source = wrap(me_s + k, samp_n)
                pltpu.make_async_copy(
                    shared.at[source, i], shared.at[source, i], xr_sem.at[source, i]
                ).wait()
            for n, (p, q) in enumerate(pairs):
                term = gram_of(shared[p, i], shared[q, i])
                cross[n] = term if cross[n] is None else cross[n] + term
        fill(1, jnp.concatenate(cross, axis=0) if len(cross) > 1 else cross[0])
        scatter_out(1)

    for copy in small_loads:
        copy.wait()
    for k in range(1, samp_n):
        source = wrap(me_s + k, samp_n)
        for n, (_, target) in enumerate(smalls):
            pltpu.make_async_copy(target.at[source], target.at[source], mr_sem.at[source, n]).wait()
    every = range(samp_n)
    signs = [lab_all[p].astype(jnp.float32) for p in every]
    alpha = [alp_all[p] for p in every]
    row_id = lax.broadcasted_iota(jnp.int32, (rows, rows), 0)
    col_id = lax.broadcasted_iota(jnp.int32, (rows, rows), 1)
    place = [
        [
            jnp.sum(
                jnp.where(ord_all[p, r : r + 1, :] == row_id, col_id, 0).astype(jnp.float32),
                axis=1, keepdims=True,
            )
            for p in every
        ]
        for r in range(ROUNDS)
    ]

    for group in range(len(part)):
        inbox[me_f, pl.ds(starts[group], slabs[group])] = part[group][me_f]
        for k in range(1, feat_n):
            source = wrap(me_f + k, feat_n)
            landed = inbox.at[source, pl.ds(starts[group], slabs[group])]
            pltpu.make_async_copy(landed, landed, rs_recv.at[group, source]).wait()
    summed = inbox[0]
    for n in range(1, feat_n):
        summed = summed + inbox[n]
    full[me_s, me_f] = summed
    gather = []
    for k in range(1, feat_n):
        target = wrap(me_f + k, feat_n)
        copy = pltpu.make_async_remote_copy(
            full.at[me_s, me_f], full.at[me_s, me_f],
            ag_send.at[k - 1], ag_recv.at[me_f], device_id={"feat": target},
        )
        copy.start()
        gather.append(copy)
    for k in range(1, feat_n):
        source = wrap(me_f + k, feat_n)
        landed = full.at[me_s, source]
        pltpu.make_async_copy(landed, landed, ag_recv.at[source]).wait()
    forward = []
    for k in range(1, samp_n):
        copy = pltpu.make_async_remote_copy(
            full.at[me_s], full.at[me_s], fw_send.at[k - 1], fw_recv.at[me_s],
            device_id={"samp": wrap(me_s + k, samp_n)},
        )
        copy.start()
        forward.append(copy)
    for k in range(1, samp_n):
        source = wrap(me_s + k, samp_n)
        pltpu.make_async_copy(full.at[source], full.at[source], fw_recv.at[source]).wait()

    def put(p, q, value):
        high = value.astype(jnp.bfloat16)
        low = (value - high.astype(jnp.float32)).astype(jnp.bfloat16)
        ghl[q, pl.ds(p * rows, rows), pl.ds(0, rows)] = high
        ghl[q, pl.ds(p * rows, rows), pl.ds(rows, rows)] = low

    gain = []
    for p in every:
        block = full[p, :, :slab_a, :].reshape(feat_n * slab_a, rows)[:rows]
        put(p, p, block)
        norm = jnp.sum(jnp.where(row_id == col_id, block, 0.0), axis=1, keepdims=True) + 1.0
        gain.append(lam_total / norm)
    if pairs:
        cross_sum = full[0, :, slab_a:, :]
        for s in range(1, samp_n):
            cross_sum = cross_sum + full[s, :, slab_a:, :]
        cross_sum = cross_sum.reshape(feat_n * slab_b, rows)
        for n, (p, q) in enumerate(pairs):
            block = cross_sum[n * rows : (n + 1) * rows]
            put(p, q, block)
            put(q, p, block.T)

    def apply(p, change):
        return jnp.dot(
            ghl[p], jnp.concatenate([change, change], axis=0), preferred_element_type=jnp.float32
        ) * (1.0 / lam_total)

    base = None
    for p in every:
        term = apply(p, (alpha[p] * signs[p]).astype(jnp.bfloat16))
        base = term if base is None else base + term
    for r in range(ROUNDS):
        local = list(alpha)
        coupled = [None] * samp_n
        moved = None
        for b in range(rows // BLOCK):
            for p in every:
                margins = base[p * rows : (p + 1) * rows]
                if coupled[p] is not None:
                    margins = margins + coupled[p]
                updated = jnp.clip(local[p] + gain[p] * (1.0 - signs[p] * margins), 0.0, 1.0)
                inside = (place[r][p] >= b * BLOCK) & (place[r][p] < (b + 1) * BLOCK)
                updated = jnp.where(inside, updated, local[p])
                change = ((updated - local[p]) * signs[p]).astype(jnp.bfloat16)
                local[p] = updated
                term = apply(p, change)
                mine = term[p * rows : (p + 1) * rows]
                coupled[p] = mine if coupled[p] is None else coupled[p] + mine
                moved = term if moved is None else moved + term
        base = base + moved * (1.0 / samp_n)
        alpha = [alpha[p] + (local[p] - alpha[p]) * (1.0 / samp_n) for p in every]

    alpha_mine, score_mine = alpha[0], base[:rows]
    for p in range(1, samp_n):
        alpha_mine = jnp.where(me_s == p, alpha[p], alpha_mine)
        score_mine = jnp.where(me_s == p, base[p * rows : (p + 1) * rows], score_mine)
    alpha_out[...] = alpha_mine
    score_out[...] = score_mine

    for copy in exchange + scatter + gather + forward:
        copy.wait_send()


def per_device(features, labels, alpha_start, order):
    rows, depth = features.shape
    label_n = labels.shape[1]
    feat_n, samp_n = lax.axis_size("feat"), lax.axis_size("samp")
    width = depth // samp_n
    piece = width // PIECES
    pair_n = samp_n * (samp_n - 1) // 2
    sizes = [round_up(-(-rows // feat_n), 8)]
    if pair_n:
        sizes.append(round_up(-(-pair_n * rows // feat_n), 8))
    lam_total = REG_SCALE * depth * feat_n
    dma = pltpu.SemaphoreType.DMA
    others, peers = max(samp_n - 1, 1), max(feat_n - 1, 1)
    return pl.pallas_call(
        functools.partial(kernel, feat_n, samp_n, lam_total),
        out_shape=[jax.ShapeDtypeStruct((rows, label_n), jnp.float32)] * 2,
        in_specs=[pl.BlockSpec(memory_space=pl.ANY)] * 4,
        out_specs=[pl.BlockSpec(memory_space=pltpu.VMEM)] * 2,
        scratch_shapes=[
            pltpu.VMEM((others, PIECES, rows, piece), features.dtype),
            pltpu.VMEM((samp_n, PIECES, rows, piece), features.dtype),
            pltpu.VMEM((samp_n,) + labels.shape, labels.dtype),
            pltpu.VMEM((samp_n,) + alpha_start.shape, jnp.float32),
            pltpu.VMEM((samp_n,) + order.shape, order.dtype),
            [pltpu.VMEM((feat_n, size, rows), jnp.float32) for size in sizes],
            pltpu.VMEM((feat_n, sum(sizes), rows), jnp.float32),
            pltpu.VMEM((samp_n, feat_n, sum(sizes), rows), jnp.float32),
            pltpu.VMEM((samp_n, samp_n * rows, 2 * rows), jnp.bfloat16),
            dma((samp_n * PIECES + 3,)),
            dma((others, PIECES)),
            dma((samp_n, PIECES)),
            dma((others, 3)),
            dma((samp_n, 3)),
            dma((2, peers)),
            dma((2, feat_n)),
            dma((peers,)),
            dma((feat_n,)),
            dma((others,)),
            dma((samp_n,)),
        ],
        compiler_params=pltpu.CompilerParams(
            collective_id=0, has_side_effects=True, vmem_limit_bytes=48 * 1024 * 1024
        ),
    )(features, labels, alpha_start, order)


def solution(mesh):
    return jax.shard_map(
        per_device,
        mesh=mesh,
        in_specs=(P("samp", "feat"), P("samp", None), P("samp", None), P(None, "samp")),
        out_specs=(P("samp", None), P("samp", None)),
        check_vma=False,
    )
```

time: 438 us -> 28.6 us (0.07)
  the two profiles are of different devices: /device:TPU:0 before, /device:TPU:1 now
where the time goes in v1:
time: 28.6 us; the launch traced here: 28.2 us
  Pallas kernels  22.3 us (78%)
  local copies, waits for them, and re-layouts  5.26 us (18%)
  between operations  0.65 us (2%)
    pallas_call x1, Pallas kernels, per_device(): pl.pallas_call(functools.partial(kernel, feat_n, samp_n, lam_total), out_...  22.3 us
    unnamed x6, local copies, waits for them, and re-layouts  3.9 us
    pallas_call x2, local copies, waits for them, and re-layouts, per_device(): pl.pallas_call(functools.partial(kernel, feat_n, samp_n, lam_total), out_...  1.36 us

profile of v1, /device:TPU:1, one launch (start us, length us, event | category | flops | bytes accessed | tf_op | source)
XLA Modules:
  0.0 28.2 jit_solution(4050948707543482149)
XLA Ops:
  0.6 0.8 %copy.6.labels = s32[128,32]{1,0:T(8,128)S(1)} copy(s32[128,32]{0,1:T(8,128)} %param.5) | data formatting | bytes 32768 | tf_op args[1]
  1.4 0.8 %copy.7.alphas = f32[128,32]{1,0:T(8,128)S(1)} copy(f32[128,32]{0,1:T(8,128)} %param.6) | data formatting | bytes 32768 | tf_op args[2]
  2.3 0.0 copy-start
  2.3 1.6 %copy-done = bf16[128,8192]{1,0:T(8,128)(2,1)S(1)} copy-done((bf16[128,8192]{1,0:T(8,128)(2,1)S(1)}, bf16[128,8192]{1,0:T(8,128)(2,1)}, u32[]{:S(2)}) %copy-start) | copy-done | bytes 2097176
  3.9 0.0 copy-start.1
  3.9 0.7 %copy-done.1 = s32[2,128]{1,0:T(2,128)S(1)} copy-done((s32[2,128]{1,0:T(2,128)S(1)}, s32[2,128]{1,0:T(2,128)}, u32[]{:S(2)}) %copy-start.1) | copy-done | bytes 1048
  4.5 22.3 %shard_map.59 = (f32[128,32]{1,0:T(8,128)S(1)}, f32[128,32]{1,0:T(8,128)S(1)}) custom-call(bf16[128,8192]{1,0:T(8,128)(2,1)S(1)} %copy-done, s32[128,32]{1,0:T(8,128)S(1)} %copy.6.labels, f32[128,32]{1,0:T(8,128)S(1)} %copy.7.alphas, s32[2,128]{1,0:T(2,128)S(1)} %copy-done.1), custom_call_target="tpu_custom_call" | custom-call | tf_op jit(solution)/shard_map/pallas_call | solution.py:278
  26.9 0.7 %copy.8 = f32[128,32]{0,1:T(8,128)} copy(f32[128,32]{1,0:T(8,128)S(1)} %get-tuple-element.2) | data formatting | bytes 32768 | tf_op jit(solution)/shard_map/pallas_call | solution.py:278
  27.6 0.7 %copy.9 = f32[128,32]{0,1:T(8,128)} copy(f32[128,32]{1,0:T(8,128)S(1)} %get-tuple-element.3) | data formatting | bytes 32768 | tf_op jit(solution)/shard_map/pallas_call | solution.py:278
Async XLA Ops:
  2.3 1.6 %copy-start = (bf16[128,8192]{1,0:T(8,128)(2,1)S(1)}, bf16[128,8192]{1,0:T(8,128)(2,1)}, u32[]{:S(2)}) copy-start(bf16[128,8192]{1,0:T(8,128)(2,1)} %feats.1) | copy-start | bytes 6291460
  3.9 0.7 %copy-start.1 = (s32[2,128]{1,0:T(2,128)S(1)}, s32[2,128]{1,0:T(2,128)}, u32[]{:S(2)}) copy-start(s32[2,128]{1,0:T(2,128)} %orders.1) | copy-start | bytes 3076

commit v2 on v1

--- a/solution.py
+++ b/solution.py
@@ -153,12 +153,12 @@
     alpha = [alp_all[p] for p in every]
     row_id = lax.broadcasted_iota(jnp.int32, (rows, rows), 0)
     col_id = lax.broadcasted_iota(jnp.int32, (rows, rows), 1)
+    block_id = (lax.broadcasted_iota(jnp.int32, (8, rows), 1) // BLOCK).astype(jnp.bfloat16)
     place = [
         [
-            jnp.sum(
-                jnp.where(ord_all[p, r : r + 1, :] == row_id, col_id, 0).astype(jnp.float32),
-                axis=1, keepdims=True,
-            )
+            gram_of(
+                block_id, jnp.where(ord_all[p, r : r + 1, :] == row_id, 1.0, 0.0).astype(jnp.bfloat16)
+            )[:1]
             for p in every
         ]
         for r in range(ROUNDS)
@@ -202,14 +202,14 @@
     def put(p, q, value):
         high = value.astype(jnp.bfloat16)
         low = (value - high.astype(jnp.float32)).astype(jnp.bfloat16)
-        ghl[q, pl.ds(p * rows, rows), pl.ds(0, rows)] = high
-        ghl[q, pl.ds(p * rows, rows), pl.ds(rows, rows)] = low
+        ghl[p, pl.ds(0, rows), pl.ds(q * rows, rows)] = high
+        ghl[p, pl.ds(rows, rows), pl.ds(q * rows, rows)] = low
 
     gain = []
     for p in every:
         block = full[p, :, :slab_a, :].reshape(feat_n * slab_a, rows)[:rows]
         put(p, p, block)
-        norm = jnp.sum(jnp.where(row_id == col_id, block, 0.0), axis=1, keepdims=True) + 1.0
+        norm = jnp.sum(jnp.where(row_id == col_id, block, 0.0), axis=0, keepdims=True) + 1.0
         gain.append(lam_total / norm)
     if pairs:
         cross_sum = full[0, :, slab_a:, :]
@@ -223,7 +223,7 @@
 
     def apply(p, change):
         return jnp.dot(
-            ghl[p], jnp.concatenate([change, change], axis=0), preferred_element_type=jnp.float32
+            jnp.concatenate([change, change], axis=1), ghl[p], preferred_element_type=jnp.float32
         ) * (1.0 / lam_total)
 
     base = None
@@ -236,25 +236,24 @@
         moved = None
         for b in range(rows // BLOCK):
             for p in every:
-                margins = base[p * rows : (p + 1) * rows]
+                margins = base[:, p * rows : (p + 1) * rows]
                 if coupled[p] is not None:
                     margins = margins + coupled[p]
                 updated = jnp.clip(local[p] + gain[p] * (1.0 - signs[p] * margins), 0.0, 1.0)
-                inside = (place[r][p] >= b * BLOCK) & (place[r][p] < (b + 1) * BLOCK)
-                updated = jnp.where(inside, updated, local[p])
+                updated = jnp.where(place[r][p] == float(b), updated, local[p])
                 change = ((updated - local[p]) * signs[p]).astype(jnp.bfloat16)
                 local[p] = updated
                 term = apply(p, change)
-                mine = term[p * rows : (p + 1) * rows]
+                mine = term[:, p * rows : (p + 1) * rows]
                 coupled[p] = mine if coupled[p] is None else coupled[p] + mine
                 moved = term if moved is None else moved + term
         base = base + moved * (1.0 / samp_n)
         alpha = [alpha[p] + (local[p] - alpha[p]) * (1.0 / samp_n) for p in every]
 
-    alpha_mine, score_mine = alpha[0], base[:rows]
+    alpha_mine, score_mine = alpha[0], base[:, :rows]
     for p in range(1, samp_n):
         alpha_mine = jnp.where(me_s == p, alpha[p], alpha_mine)
-        score_mine = jnp.where(me_s == p, base[p * rows : (p + 1) * rows], score_mine)
+        score_mine = jnp.where(me_s == p, base[:, p * rows : (p + 1) * rows], score_mine)
     alpha_out[...] = alpha_mine
     score_out[...] = score_mine
 
@@ -265,6 +264,7 @@
 def per_device(features, labels, alpha_start, order):
     rows, depth = features.shape
     label_n = labels.shape[1]
+    labels, alpha_start = labels.T, alpha_start.T
     feat_n, samp_n = lax.axis_size("feat"), lax.axis_size("samp")
     width = depth // samp_n
     piece = width // PIECES
@@ -275,10 +275,10 @@
     lam_total = REG_SCALE * depth * feat_n
     dma = pltpu.SemaphoreType.DMA
     others, peers = max(samp_n - 1, 1), max(feat_n - 1, 1)
-    return pl.pallas_call(
+    alpha, scores = pl.pallas_call(
         functools.partial(kernel, feat_n, samp_n, lam_total),
-        out_shape=[jax.ShapeDtypeStruct((rows, label_n), jnp.float32)] * 2,
-        in_specs=[pl.BlockSpec(memory_space=pl.ANY)] * 4,
+        out_shape=[jax.ShapeDtypeStruct((label_n, rows), jnp.float32)] * 2,
+        in_specs=[pl.BlockSpec(memory_space=pltpu.HBM)] * 4,
         out_specs=[pl.BlockSpec(memory_space=pltpu.VMEM)] * 2,
         scratch_shapes=[
             pltpu.VMEM((others, PIECES, rows, piece), features.dtype),
@@ -289,7 +289,7 @@
             [pltpu.VMEM((feat_n, size, rows), jnp.float32) for size in sizes],
             pltpu.VMEM((feat_n, sum(sizes), rows), jnp.float32),
             pltpu.VMEM((samp_n, feat_n, sum(sizes), rows), jnp.float32),
-            pltpu.VMEM((samp_n, samp_n * rows, 2 * rows), jnp.bfloat16),
+            pltpu.VMEM((samp_n, 2 * rows, samp_n * rows), jnp.bfloat16),
             dma((samp_n * PIECES + 3,)),
             dma((others, PIECES)),
             dma((samp_n, PIECES)),
@@ -303,9 +303,10 @@
             dma((samp_n,)),
         ],
         compiler_params=pltpu.CompilerParams(
-            collective_id=0, has_side_effects=True, vmem_limit_bytes=48 * 1024 * 1024
+            collective_id=0, has_side_effects=True, vmem_limit_bytes=65000000
         ),
     )(features, labels, alpha_start, order)
+    return alpha.T, scores.T
 
 
 def solution(mesh):

time: 28.6 us -> 26.4 us (0.923)
  local copies, waits for them, and re-layouts: 5.26 us -> 2.65 us
  Pallas kernels: 22.3 us -> 22.8 us
    pallas_call x2 -> x0, local copies, waits for them, and re-layouts: 1.36 us -> none  [per_device(): pl.pallas_call(functools.partial(kernel, feat_n, samp_n, lam_total), out_...]
    unnamed x6 -> x2, local copies, waits for them, and re-layouts: 3.9 us -> 2.65 us
    pallas_call x1, Pallas kernels: 22.3 us -> 22.8 us  [per_device(): pl.pallas_call(functools.partial(kernel, feat_n, samp_n, lam_total), out_...]
where the time goes in v2:
time: 26.4 us; the launch traced here: 26.1 us
  Pallas kernels  22.8 us (86%)
  local copies, waits for them, and re-layouts  2.65 us (10%)
  between operations  0.64 us (2%)
    pallas_call x1, Pallas kernels, per_device(): pl.pallas_call(functools.partial(kernel, feat_n, samp_n, lam_total), out_...  22.8 us
    unnamed x2, local copies, waits for them, and re-layouts  2.65 us

profile of v2, /device:TPU:1, one launch (start us, length us, event | category | flops | bytes accessed | tf_op | source)
XLA Modules:
  0.0 26.1 jit_solution(11868048340300547507)
XLA Ops:
  0.6 22.8 %shard_map.59 = (f32[32,128]{1,0:T(8,128)}, f32[32,128]{1,0:T(8,128)}) custom-call(bf16[128,8192]{1,0:T(8,128)(2,1)} %feats.1, s32[32,128]{1,0:T(8,128)} %bitcast.4, f32[32,128]{1,0:T(8,128)} %bitcast.5, s32[2,128]{1,0:T(2,128)} %orders.1), custom_call_target="tpu_custom_call" | custom-call | tf_op jit(solution)/shard_map/pallas_call | solution.py:278
  23.5 1.3 %copy.8 = f32[128,32]{0,1:T(8,128)} copy(f32[128,32]{0,1:T(8,128)} %bitcast.7) | data formatting | bytes 32768
  24.8 1.3 %copy.9 = f32[128,32]{0,1:T(8,128)} copy(f32[128,32]{0,1:T(8,128)} %bitcast.6) | data formatting | bytes 32768

commit v3 on v2

--- a/solution.py
+++ b/solution.py
@@ -11,6 +11,7 @@
 ROUNDS = 2
 REG_SCALE = 0.9
 PIECES = 2
+KINDS = (jnp.float32, jnp.bfloat16)
 
 
 def round_up(value, unit):
@@ -32,7 +33,7 @@
     feats, labels, alphas, orders,
     alpha_out, score_out,
     own, shared, lab_all, alp_all, ord_all, part, inbox, full, ghl,
-    load_sem, xs_sem, xr_sem, ms_sem, mr_sem, rs_send, rs_recv, ag_send, ag_recv, fw_send, fw_recv,
+    here_sem, group_sem, go_sem, load_sem, xs_sem, xr_sem, ms_sem, mr_sem, rs_send, rs_recv, ag_send, ag_recv, fw_send, fw_recv,
 ):
     rows, depth = feats.shape
     width = depth // samp_n
@@ -40,15 +41,10 @@
     slab_a = part[0].shape[1]
     slab_b = part[1].shape[1] if len(part) > 1 else 0
     slabs = (slab_a, slab_b)
-    starts = (0, slab_a)
+    lead = samp_n - 1
     me_f, me_s = lax.axis_index("feat"), lax.axis_index("samp")
 
     barrier = pltpu.get_barrier_semaphore()
-    for k in range(1, samp_n):
-        pl.semaphore_signal(barrier, inc=1, device_id={"samp": wrap(me_s + k, samp_n)})
-    for k in range(1, feat_n):
-        pl.semaphore_signal(barrier, inc=1, device_id={"feat": wrap(me_f + k, feat_n)})
-
     def columns(owner, index):
         return pl.ds(pl.multiple_of(owner * width + index * piece, 128), piece)
 
@@ -70,7 +66,31 @@
     for copy in small_loads:
         copy.start()
 
-    pl.semaphore_wait(barrier, samp_n - 1 + feat_n - 1)
+    if samp_n > 1:
+        @pl.when(me_s == lead)
+        def _():
+            for q in range(samp_n - 1):
+                pl.semaphore_signal(barrier, inc=1, device_id={"samp": q})
+
+        @pl.when(me_s != lead)
+        def _():
+            pl.semaphore_wait(barrier, 1)
+            pl.semaphore_signal(here_sem, inc=1, device_id={"samp": lead})
+
+    @pl.when(me_s == lead)
+    def _():
+        if samp_n > 1:
+            pl.semaphore_wait(here_sem, samp_n - 1)
+        for k in range(1, feat_n):
+            pl.semaphore_signal(barrier, inc=1, device_id={"feat": wrap(me_f + k, feat_n)})
+        if samp_n > 2:
+            for q in range(samp_n - 1):
+                pl.semaphore_signal(group_sem, inc=1, device_id={"samp": q})
+
+    if samp_n > 2:
+        @pl.when(me_s != lead)
+        def _():
+            pl.semaphore_wait(group_sem, 1)
 
     exchange = []
     for k in range(1, samp_n):
@@ -102,14 +122,25 @@
             term = gram_of(block, block)
             total = term if total is None else total + term
 
+    @pl.when(me_s == lead)
+    def _():
+        if feat_n > 1:
+            pl.semaphore_wait(barrier, feat_n - 1)
+        for q in range(samp_n - 1):
+            pl.semaphore_signal(go_sem, inc=1, device_id={"samp": q})
+
+    if samp_n > 1:
+        @pl.when(me_s != lead)
+        def _():
+            pl.semaphore_wait(go_sem, 1)
+
     scatter = []
 
     def scatter_out(group):
-        size, start = slabs[group], starts[group]
         for k in range(1, feat_n):
             target = wrap(me_f + k, feat_n)
             copy = pltpu.make_async_remote_copy(
-                part[group].at[target], inbox.at[me_f, pl.ds(start, size)],
+                part[group].at[target], inbox[group].at[me_f],
                 rs_send.at[group, k - 1], rs_recv.at[group, me_f], device_id={"feat": target},
             )
             copy.start()
@@ -122,7 +153,7 @@
             value = jnp.concatenate(
                 [value, jnp.zeros((count - value.shape[0], rows), jnp.float32)], axis=0
             )
-        part[group][...] = value.reshape(feat_n, size, rows)
+        part[group][...] = value.reshape(feat_n, size, rows).astype(part[group].dtype)
 
     fill(0, total)
     scatter_out(0)
@@ -164,40 +195,52 @@
         for r in range(ROUNDS)
     ]
 
-    for group in range(len(part)):
-        inbox[me_f, pl.ds(starts[group], slabs[group])] = part[group][me_f]
+    gather, forward = [], []
+
+    def sum_and_gather(group):
+        inbox[group][me_f] = part[group][me_f]
+        for k in range(1, feat_n):
+            landed = inbox[group].at[wrap(me_f + k, feat_n)]
+            pltpu.make_async_copy(landed, landed, rs_recv.at[group, wrap(me_f + k, feat_n)]).wait()
+        summed = inbox[group][0].astype(jnp.float32)
+        for n in range(1, feat_n):
+            summed = summed + inbox[group][n].astype(jnp.float32)
+        full[group][me_s, me_f] = summed.astype(full[group].dtype)
+        for k in range(1, feat_n):
+            copy = pltpu.make_async_remote_copy(
+                full[group].at[me_s, me_f], full[group].at[me_s, me_f],
+                ag_send.at[group, k - 1], ag_recv.at[group, me_f],
+                device_id={"feat": wrap(me_f + k, feat_n)},
+            )
+            copy.start()
+            gather.append(copy)
+
+    def pass_on(group):
         for k in range(1, feat_n):
             source = wrap(me_f + k, feat_n)
-            landed = inbox.at[source, pl.ds(starts[group], slabs[group])]
-            pltpu.make_async_copy(landed, landed, rs_recv.at[group, source]).wait()
-    summed = inbox[0]
-    for n in range(1, feat_n):
-        summed = summed + inbox[n]
-    full[me_s, me_f] = summed
-    gather = []
-    for k in range(1, feat_n):
-        target = wrap(me_f + k, feat_n)
-        copy = pltpu.make_async_remote_copy(
-            full.at[me_s, me_f], full.at[me_s, me_f],
-            ag_send.at[k - 1], ag_recv.at[me_f], device_id={"feat": target},
-        )
-        copy.start()
-        gather.append(copy)
-    for k in range(1, feat_n):
-        source = wrap(me_f + k, feat_n)
-        landed = full.at[me_s, source]
-        pltpu.make_async_copy(landed, landed, ag_recv.at[source]).wait()
-    forward = []
-    for k in range(1, samp_n):
-        copy = pltpu.make_async_remote_copy(
-            full.at[me_s], full.at[me_s], fw_send.at[k - 1], fw_recv.at[me_s],
-            device_id={"samp": wrap(me_s + k, samp_n)},
-        )
-        copy.start()
-        forward.append(copy)
-    for k in range(1, samp_n):
-        source = wrap(me_s + k, samp_n)
-        pltpu.make_async_copy(full.at[source], full.at[source], fw_recv.at[source]).wait()
+            landed = full[group].at[me_s, source]
+            pltpu.make_async_copy(landed, landed, ag_recv.at[group, source]).wait()
+        for k in range(1, samp_n):
+            copy = pltpu.make_async_remote_copy(
+                full[group].at[me_s], full[group].at[me_s],
+                fw_send.at[group, k - 1], fw_recv.at[group, me_s],
+                device_id={"samp": wrap(me_s + k, samp_n)},
+            )
+            copy.start()
+            forward.append(copy)
+
+    def arrived(group):
+        for k in range(1, samp_n):
+            source = wrap(me_s + k, samp_n)
+            landed = full[group].at[source]
+            pltpu.make_async_copy(landed, landed, fw_recv.at[group, source]).wait()
+
+    groups = range(len(part))
+    for group in groups:
+        sum_and_gather(group)
+    for group in groups:
+        pass_on(group)
+    arrived(0)
 
     def put(p, q, value):
         high = value.astype(jnp.bfloat16)
@@ -207,14 +250,15 @@
 
     gain = []
     for p in every:
-        block = full[p, :, :slab_a, :].reshape(feat_n * slab_a, rows)[:rows]
+        block = full[0][p].reshape(feat_n * slab_a, rows)[:rows]
         put(p, p, block)
         norm = jnp.sum(jnp.where(row_id == col_id, block, 0.0), axis=0, keepdims=True) + 1.0
         gain.append(lam_total / norm)
     if pairs:
-        cross_sum = full[0, :, slab_a:, :]
+        arrived(1)
+        cross_sum = full[1][0].astype(jnp.float32)
         for s in range(1, samp_n):
-            cross_sum = cross_sum + full[s, :, slab_a:, :]
+            cross_sum = cross_sum + full[1][s].astype(jnp.float32)
         cross_sum = cross_sum.reshape(feat_n * slab_b, rows)
         for n, (p, q) in enumerate(pairs):
             block = cross_sum[n * rows : (n + 1) * rows]
@@ -286,10 +330,13 @@
             pltpu.VMEM((samp_n,) + labels.shape, labels.dtype),
             pltpu.VMEM((samp_n,) + alpha_start.shape, jnp.float32),
             pltpu.VMEM((samp_n,) + order.shape, order.dtype),
-            [pltpu.VMEM((feat_n, size, rows), jnp.float32) for size in sizes],
-            pltpu.VMEM((feat_n, sum(sizes), rows), jnp.float32),
-            pltpu.VMEM((samp_n, feat_n, sum(sizes), rows), jnp.float32),
+            [pltpu.VMEM((feat_n, size, rows), kind) for size, kind in zip(sizes, KINDS)],
+            [pltpu.VMEM((feat_n, size, rows), kind) for size, kind in zip(sizes, KINDS)],
+            [pltpu.VMEM((samp_n, feat_n, size, rows), kind) for size, kind in zip(sizes, KINDS)],
             pltpu.VMEM((samp_n, 2 * rows, samp_n * rows), jnp.bfloat16),
+            pltpu.SemaphoreType.REGULAR,
+            pltpu.SemaphoreType.REGULAR,
+            pltpu.SemaphoreType.REGULAR,
             dma((samp_n * PIECES + 3,)),
             dma((others, PIECES)),
             dma((samp_n, PIECES)),
@@ -297,13 +344,13 @@
             dma((samp_n, 3)),
             dma((2, peers)),
             dma((2, feat_n)),
-            dma((peers,)),
-            dma((feat_n,)),
-            dma((others,)),
-            dma((samp_n,)),
+            dma((2, peers)),
+            dma((2, feat_n)),
+            dma((2, others)),
+            dma((2, samp_n)),
         ],
         compiler_params=pltpu.CompilerParams(
-            collective_id=0, has_side_effects=True, vmem_limit_bytes=65000000
+            collective_id=0, has_side_effects=True, vmem_limit_bytes=56000000
         ),
     )(features, labels, alpha_start, order)
     return alpha.T, scores.T

time: 26.4 us -> 24.7 us (0.936)
  Pallas kernels: 22.8 us -> 20.4 us
  local copies, waits for them, and re-layouts: 2.65 us -> 3.32 us
    pallas_call x1, Pallas kernels: 22.8 us -> 20.4 us  [per_device(): pl.pallas_call(functools.partial(kernel, feat_n, samp_n, lam_total), out_...]
    unnamed x2 -> x8, local copies, waits for them, and re-layouts: 2.65 us -> 3.32 us
where the time goes in v3:
time: 24.7 us; the launch traced here: 24.3 us
  Pallas kernels  20.4 us (83%)
  local copies, waits for them, and re-layouts  3.32 us (13%)
  between operations  0.65 us (3%)
    pallas_call x1, Pallas kernels, per_device(): pl.pallas_call(functools.partial(kernel, feat_n, samp_n, lam_total), out_...  20.4 us
    unnamed x8, local copies, waits for them, and re-layouts  3.32 us

profile of v3, /device:TPU:1, one launch (start us, length us, event | category | flops | bytes accessed | tf_op | source)
XLA Modules:
  0.0 24.3 jit_solution(17351134677396036537)
XLA Ops:
  0.6 0.0 copy-start
  0.6 0.7 %copy-done = s32[128,32]{0,1:T(8,128)S(1)} copy-done((s32[128,32]{0,1:T(8,128)S(1)}, s32[128,32]{0,1:T(8,128)}, u32[]{:S(2)}) %copy-start) | copy-done | bytes 16408
  1.3 0.0 copy-start.1
  1.4 0.7 %copy-done.1 = f32[128,32]{0,1:T(8,128)S(1)} copy-done((f32[128,32]{0,1:T(8,128)S(1)}, f32[128,32]{0,1:T(8,128)}, u32[]{:S(2)}) %copy-start.1) | copy-done | bytes 16408
  2.1 0.0 copy-start.2
  2.1 0.7 %copy-done.2 = s32[2,128]{1,0:T(2,128)S(1)} copy-done((s32[2,128]{1,0:T(2,128)S(1)}, s32[2,128]{1,0:T(2,128)}, u32[]{:S(2)}) %copy-start.2) | copy-done | bytes 1048
  2.7 20.4 %shard_map.59 = (f32[32,128]{1,0:T(8,128)S(1)}, f32[32,128]{1,0:T(8,128)S(1)}) custom-call(bf16[128,8192]{1,0:T(8,128)(2,1)} %feats.1, s32[32,128]{1,0:T(8,128)S(1)} %bitcast.4, f32[32,128]{1,0:T(8,128)S(1)} %bitcast.5, s32[2,128]{1,0:T(2,128)S(1)} %copy-done.2), custom_call_target="tpu_custom_call" | custom-call | tf_op jit(solution)/shard_map/pallas_call | solution.py:322
  23.1 0.6 %copy.8 = f32[128,32]{0,1:T(8,128)} copy(f32[128,32]{0,1:T(8,128)S(1)} %bitcast.7) | data formatting | bytes 32768
  23.7 0.6 %copy.9 = f32[128,32]{0,1:T(8,128)} copy(f32[128,32]{0,1:T(8,128)S(1)} %bitcast.6) | data formatting | bytes 32768
Async XLA Ops:
  0.6 0.7 %copy-start = (s32[128,32]{0,1:T(8,128)S(1)}, s32[128,32]{0,1:T(8,128)}, u32[]{:S(2)}) copy-start(s32[128,32]{0,1:T(8,128)} %param.5) | copy-start | bytes 49156
  1.3 0.7 %copy-start.1 = (f32[128,32]{0,1:T(8,128)S(1)}, f32[128,32]{0,1:T(8,128)}, u32[]{:S(2)}) copy-start(f32[128,32]{0,1:T(8,128)} %param.6) | copy-start | bytes 49156
  2.1 0.7 %copy-start.2 = (s32[2,128]{1,0:T(2,128)S(1)}, s32[2,128]{1,0:T(2,128)}, u32[]{:S(2)}) copy-start(s32[2,128]{1,0:T(2,128)} %orders.1) | copy-start | bytes 3076

commit v4 on v3

--- a/solution.py
+++ b/solution.py
@@ -122,18 +122,6 @@
             term = gram_of(block, block)
             total = term if total is None else total + term
 
-    @pl.when(me_s == lead)
-    def _():
-        if feat_n > 1:
-            pl.semaphore_wait(barrier, feat_n - 1)
-        for q in range(samp_n - 1):
-            pl.semaphore_signal(go_sem, inc=1, device_id={"samp": q})
-
-    if samp_n > 1:
-        @pl.when(me_s != lead)
-        def _():
-            pl.semaphore_wait(go_sem, 1)
-
     scatter = []
 
     def scatter_out(group):
@@ -156,7 +144,6 @@
         part[group][...] = value.reshape(feat_n, size, rows).astype(part[group].dtype)
 
     fill(0, total)
-    scatter_out(0)
 
     pairs = [(p, q) for p in range(samp_n) for q in range(p + 1, samp_n)]
     if pairs:
@@ -171,7 +158,21 @@
                 term = gram_of(shared[p, i], shared[q, i])
                 cross[n] = term if cross[n] is None else cross[n] + term
         fill(1, jnp.concatenate(cross, axis=0) if len(cross) > 1 else cross[0])
-        scatter_out(1)
+
+    @pl.when(me_s == lead)
+    def _():
+        if feat_n > 1:
+            pl.semaphore_wait(barrier, feat_n - 1)
+        for q in range(samp_n - 1):
+            pl.semaphore_signal(go_sem, inc=1, device_id={"samp": q})
+
+    if samp_n > 1:
+        @pl.when(me_s != lead)
+        def _():
+            pl.semaphore_wait(go_sem, 1)
+
+    for group in reversed(range(len(part))):
+        scatter_out(group)
 
     for copy in small_loads:
         copy.wait()
@@ -352,7 +353,7 @@
         compiler_params=pltpu.CompilerParams(
             collective_id=0, has_side_effects=True, vmem_limit_bytes=56000000
         ),
-    )(features, labels, alpha_start, order)
+    )(*(pltpu.with_memory_space_constraint(x, pltpu.HBM) for x in (features, labels, alpha_start, order)))
     return alpha.T, scores.T
 
 

time: 24.7 us -> 22.4 us (0.907); the launches traced: 24.3 us -> 22.3 us
  local copies, waits for them, and re-layouts: 3.32 us -> 1.21 us
    unnamed x8 -> x2, local copies, waits for them, and re-layouts: 3.32 us -> 1.21 us
where the time goes in v4:
time: 22.4 us; the launch traced here: 22.3 us
  Pallas kernels  20.4 us (91%)
  local copies, waits for them, and re-layouts  1.21 us (5%)
  between operations  0.64 us (3%)
    pallas_call x1, Pallas kernels, per_device(): pl.pallas_call(functools.partial(kernel, feat_n, samp_n, lam_total), out_...  20.4 us
    unnamed x2, local copies, waits for them, and re-layouts  1.21 us

profile of v4, /device:TPU:1, one launch (start us, length us, event | category | flops | bytes accessed | tf_op | source)
XLA Modules:
  0.0 22.3 jit_solution(3222850527658141584)
XLA Ops:
  0.6 20.4 %shard_map.59 = (f32[32,128]{1,0:T(8,128)S(1)}, f32[32,128]{1,0:T(8,128)S(1)}) custom-call(bf16[128,8192]{1,0:T(8,128)(2,1)} %feats.1, s32[32,128]{1,0:T(8,128)} %bitcast.6, f32[32,128]{1,0:T(8,128)} %bitcast.7, s32[2,128]{1,0:T(2,128)} %orders.1), custom_call_target="tpu_custom_call" | custom-call | tf_op jit(solution)/shard_map/pallas_call | solution.py:323
  21.1 0.6 %copy.8 = f32[128,32]{0,1:T(8,128)} copy(f32[128,32]{0,1:T(8,128)S(1)} %bitcast.5) | data formatting | bytes 32768
  21.7 0.6 %copy.9 = f32[128,32]{0,1:T(8,128)} copy(f32[128,32]{0,1:T(8,128)S(1)} %bitcast.4) | data formatting | bytes 32768

commit v5 on v4

--- a/solution.py
+++ b/solution.py
@@ -171,7 +171,7 @@
         def _():
             pl.semaphore_wait(go_sem, 1)
 
-    for group in reversed(range(len(part))):
+    for group in range(len(part)):
         scatter_out(group)
 
     for copy in small_loads:
@@ -207,11 +207,13 @@
         for n in range(1, feat_n):
             summed = summed + inbox[group][n].astype(jnp.float32)
         full[group][me_s, me_f] = summed.astype(full[group].dtype)
-        for k in range(1, feat_n):
+        for n in range(1, feat_n * (samp_n if group else 1)):
             copy = pltpu.make_async_remote_copy(
                 full[group].at[me_s, me_f], full[group].at[me_s, me_f],
-                ag_send.at[group, k - 1], ag_recv.at[group, me_f],
-                device_id={"feat": wrap(me_f + k, feat_n)},
+                ag_send.at[group, n], ag_recv.at[group, me_s, me_f],
+                device_id={
+                    "feat": wrap(me_f + n % feat_n, feat_n), "samp": wrap(me_s + n // feat_n, samp_n)
+                },
             )
             copy.start()
             gather.append(copy)
@@ -220,7 +222,7 @@
         for k in range(1, feat_n):
             source = wrap(me_f + k, feat_n)
             landed = full[group].at[me_s, source]
-            pltpu.make_async_copy(landed, landed, ag_recv.at[group, source]).wait()
+            pltpu.make_async_copy(landed, landed, ag_recv.at[group, me_s, source]).wait()
         for k in range(1, samp_n):
             copy = pltpu.make_async_remote_copy(
                 full[group].at[me_s], full[group].at[me_s],
@@ -230,6 +232,12 @@
             copy.start()
             forward.append(copy)
 
+    def cross_arrived():
+        for n in range(1, feat_n * samp_n):
+            from_f, from_s = wrap(me_f + n % feat_n, feat_n), wrap(me_s + n // feat_n, samp_n)
+            landed = full[1].at[from_s, from_f]
+            pltpu.make_async_copy(landed, landed, ag_recv.at[1, from_s, from_f]).wait()
+
     def arrived(group):
         for k in range(1, samp_n):
             source = wrap(me_s + k, samp_n)
@@ -239,8 +247,7 @@
     groups = range(len(part))
     for group in groups:
         sum_and_gather(group)
-    for group in groups:
-        pass_on(group)
+    pass_on(0)
     arrived(0)
 
     def put(p, q, value):
@@ -256,7 +263,7 @@
         norm = jnp.sum(jnp.where(row_id == col_id, block, 0.0), axis=0, keepdims=True) + 1.0
         gain.append(lam_total / norm)
     if pairs:
-        arrived(1)
+        cross_arrived()
         cross_sum = full[1][0].astype(jnp.float32)
         for s in range(1, samp_n):
             cross_sum = cross_sum + full[1][s].astype(jnp.float32)
@@ -345,8 +352,8 @@
             dma((samp_n, 3)),
             dma((2, peers)),
             dma((2, feat_n)),
-            dma((2, peers)),
-            dma((2, feat_n)),
+            dma((2, samp_n * feat_n)),
+            dma((2, samp_n, feat_n)),
             dma((2, others)),
             dma((2, samp_n)),
         ],

time: 22.4 us -> 22.4 us (level)
  no operation moved by 1% of the time
where the time goes in v5:
time: 22.4 us; the launch traced here: 22.3 us
  Pallas kernels  20.4 us (91%)
  local copies, waits for them, and re-layouts  1.21 us (5%)
  between operations  0.64 us (3%)
    pallas_call x1, Pallas kernels, per_device(): pl.pallas_call(functools.partial(kernel, feat_n, samp_n, lam_total), out_...  20.4 us
    unnamed x2, local copies, waits for them, and re-layouts  1.21 us

profile of v5, /device:TPU:1, one launch (start us, length us, event | category | flops | bytes accessed | tf_op | source)
XLA Modules:
  0.0 22.3 jit_solution(15073264403350156799)
XLA Ops:
  0.6 20.4 %shard_map.59 = (f32[32,128]{1,0:T(8,128)S(1)}, f32[32,128]{1,0:T(8,128)S(1)}) custom-call(bf16[128,8192]{1,0:T(8,128)(2,1)} %feats.1, s32[32,128]{1,0:T(8,128)} %bitcast.6, f32[32,128]{1,0:T(8,128)} %bitcast.7, s32[2,128]{1,0:T(2,128)} %orders.1), custom_call_target="tpu_custom_call" | custom-call | tf_op jit(solution)/shard_map/pallas_call | solution.py:330
  21.1 0.6 %copy.8 = f32[128,32]{0,1:T(8,128)} copy(f32[128,32]{0,1:T(8,128)S(1)} %bitcast.5) | data formatting | bytes 32768
  21.7 0.6 %copy.9 = f32[128,32]{0,1:T(8,128)} copy(f32[128,32]{0,1:T(8,128)S(1)} %bitcast.4) | data formatting | bytes 32768
